TPU v7x, 512 devices: a whole 4x8x8 slice. The times are simulated.
512 devices in a mesh: row: 32 (over x, y), col: 16 (over z, core).
Axes of the slice: x: 4, y: 8, z: 8, core: 2. Of those that a mesh axis runs over, the one named last changes fastest.
Arguments:
- activations: bfloat16 [2048, 16384], P('row', 'col'), may hold values from -6 to 6
- cotangents: bfloat16 [2048, 16384], P('col', 'row'), may hold values from -6 to 6
- weights: bfloat16 [16384, 16384], P('row', 'col'), may hold values from -6 to 6
- momentum: bfloat16 [16384, 16384], P('row', 'col'), may hold values from -16 to 16
- right_basis: float32 [64, 16384], P(None, 'col'), may hold values from -1 to 1
- next_inputs: bfloat16 [1024, 16384], P('row', 'col'), may hold values from -6 to 6
Outputs:
- weights_new: bfloat16 [16384, 16384], P('row', 'col')
- momentum_new: bfloat16 [16384, 16384], P('row', 'col')
- basis_new: float32 [64, 16384], P(None, 'col')
- outputs: bfloat16 [1024, 16384], P('col', 'row')
All inputs are finite; a program needn't handle non-finite values.
Results may differ from a plain program's by a relative error of at most 0.02.
Values may be sent and summed in bfloat16 or wider, within the bound.
A program may use at most 64 MiB of HBM per device.

v0:
```python
import math

import jax
import jax.numpy as jnp
from jax import lax
from jax.sharding import Mesh
from jax.sharding import PartitionSpec as P

DOUT = 16384
DIN = 16384
RANK = 64
COL = ("col_0", "col_1")


momentum_decay = 0.95
learn_rate = 0.3
norm_eps = 1e-06


def sent_to_all(x, axis):
    size = lax.axis_size(axis)
    return lax.all_to_all(jnp.broadcast_to(x[None], (size, *x.shape)), axis, 0, 0, tiled=True)


def in_order(parts, dim):
    parts = jnp.moveaxis(parts, 0, dim)
    dims = parts.shape
    return parts.reshape(*dims[:dim], dims[dim] * dims[dim + 1], *dims[dim + 2 :])


def gathered_by_axis(x, axes, dim):
    far, near = axes
    parts = sent_to_all(sent_to_all(x, far), near)
    return in_order(parts.swapaxes(0, 1).reshape(-1, *x.shape), dim)


def rows_for(lines, size):
    spare = -lines.shape[0] % size
    if not spare:
        return lines
    return jnp.concatenate([lines, jnp.zeros((spare, *lines.shape[1:]), lines.dtype)])


def collect(x, axis, dim):
    return in_order(sent_to_all(x, axis), dim)


def cut_along(x, dim, size):
    dims = x.shape
    parts = x.reshape(*dims[:dim], size, dims[dim] // size, *dims[dim + 1 :])
    return jnp.moveaxis(parts, dim, 0)


def sum_at_owner(x, axis, dim):
    size = lax.axis_size(axis)
    parts = lax.all_to_all(cut_along(x, dim, size), axis, 0, 0, tiled=True)
    return jnp.sum(parts.astype(jnp.float32), axis=0)


def nested_sum(x, axes):
    lines = x.reshape(-1, x.shape[-1])
    padded = rows_for(lines, lax.axis_size(axes))
    whole = collect(sum_at_owner(padded, axes, 0).astype(jnp.bfloat16), axes, 0)
    return lax.slice_in_dim(whole, 0, len(lines)).reshape(x.shape).astype(jnp.float32)


def taken_together(x, axis):
    everything = sent_to_all(x, axis)
    return jnp.sum(everything, axis=0)


def body(activations, cotangents, weights, momentum, right_basis, next_inputs):
    highest = lax.Precision.HIGHEST
    token_count = cotangents.shape[0] * lax.axis_size(COL)
    act_whole = lax.all_gather(activations, "row", axis=0, tiled=True)
    summed = lax.dot_general(
        gathered_by_axis(cotangents, ("col_0", "col_1"), 0),
        act_whole,
        (((0,), (0,)), ((), ())),
        preferred_element_type=jnp.float32,
    )
    gradient = summed / math.sqrt(token_count)
    buffer = momentum.astype(jnp.float32) + gradient
    left_part = lax.dot_general(right_basis, buffer, (((1,), (1,)), ((), ())), precision=highest)
    left_factor = nested_sum(left_part.astype(jnp.bfloat16), COL)
    gram_matrix = taken_together(jnp.dot(left_factor, left_factor.T, precision=highest), "row")
    factor = jnp.linalg.cholesky(gram_matrix)
    orth_basis = lax.linalg.triangular_solve(factor, left_factor, left_side=True, lower=True)
    right_factor = nested_sum(
        jnp.dot(orth_basis, buffer, precision=highest).astype(jnp.bfloat16), "row"
    )
    feedback = lax.dot_general(
        orth_basis, right_factor, (((0,), (0,)), ((), ())), precision=highest
    )
    momentum_new = (buffer - (1.0 - momentum_decay) * feedback).astype(jnp.bfloat16)
    squares = taken_together(jnp.sum(right_factor * right_factor, axis=1), COL)
    basis_new = right_factor / jnp.sqrt(squares + norm_eps)[:, None]
    update = lax.dot_general(orth_basis, basis_new, (((0,), (0,)), ((), ())), precision=highest)
    step_scale = learn_rate * math.sqrt(DOUT * DIN / RANK)
    weights_new = (weights.astype(jnp.float32) - step_scale * update).astype(jnp.bfloat16)
    next_whole = lax.all_gather(next_inputs, "row", axis=0, tiled=True)
    product = lax.dot_general(
        next_whole, weights_new, (((1,), (1,)), ((), ())), preferred_element_type=jnp.float32
    )
    outputs = sum_at_owner((product / math.sqrt(DIN)).astype(jnp.bfloat16), COL, 0).astype(
        jnp.bfloat16
    )
    return (weights_new, momentum_new, basis_new, outputs)


def solution(mesh):
    torus = Mesh(mesh.devices.reshape(mesh.shape["row"], 8, 2), ("row", "col_0", "col_1"))
    placed = (
        P("row", COL),
        P(COL, "row"),
        P("row", COL),
        P("row", COL),
        P(None, COL),
        P("row", COL),
    )
    return jax.shard_map(
        body,
        mesh=torus,
        in_specs=placed,
        out_specs=(P("row", COL), P("row", COL), P(None, COL), P(COL, "row")),
        check_vma=False,
    )
```

profile of v0, /device:TPU:1, one launch (start us, length us, event | category | flops | bytes accessed | tf_op | source)
XLA Modules:
  0.0 277.0 jit_solution(12497052277360085594)
XLA Ops:
  8.9 38.0 %all_to_all.46 = bf16[8,128,512]{2,1,0:T(8,128)(2,1)S(1)} all-to-all(bf16[8,128,512]{2,1,0:T(8,128)(2,1)S(1)} %broadcast_in_dim.15), channel_id=1, replica_groups=mesh['row'=32,'col_0'=8,'col_1'=2] {'col_0'}, dimensions={0} | all-to-all | bytes 2097152 | tf_op jit(solution)/shard_map/all_to_all | solution.py:22
  47.1 7.4 %all_to_all.47 = bf16[2,8,128,512]{3,2,1,0:T(8,128)(2,1)S(1)} all-to-all(bf16[2,8,128,512]{3,2,1,0:T(8,128)(2,1)S(1)} %broadcast_in_dim.16), channel_id=1, replica_groups=mesh['row'=32,'col_0'=8,'col_1'=2] {'col_1'}, dimensions={0} | all-to-all | bytes 4194304 | tf_op jit(solution)/shard_map/all_to_all | solution.py:22
  54.5 1.5 copy.19
  56.0 44.0 %all-gather.3.cloned.1.call-done = bf16[2048,1024]{1,0:T(8,128)(2,1)} async-done(((bf16[64,1024]{1,0:T(8,128)(2,1)}), bf16[2048,1024]{1,0:T(8,128)(2,1)}) %all-gather.3.cloned.1.call-update) | async-done | bytes 4194320 | tf_op jit(solution)/shard_map/all_gather | solution.py:75
  100.1 5.2 %multiply_add_fusion = f32[512,1024]{1,0:T(8,128)S(1)} fusion(bf16[512,1024]{1,0:T(8,128)(2,1)S(1)} %copy-done.4, bf16[2048,512]{1,0:T(8,128)(2,1)} %bitcast.34, bf16[2048,1024]{1,0:T(8,128)(2,1)} %all-gather.3.cloned.1.call-done), kind=kOutput, calls=%fused_computation.3 | convolution fusion | flops 2149056512 | bytes 9437184 | tf_op jit(solution)/shard_map/dot_general | solution.py:76
  105.3 2.2 fusion.1
  108.1 11.6 %all-to-all-start.2 = ((bf16[16,4,512]{2,1,0:T(4,128)(2,1)}), bf16[16,4,512]{2,1,0:T(4,128)(2,1)S(1)}, u32[]{:S(2)}, u32[]{:S(2)}) async-start(bf16[16,4,512]{2,1,0:T(4,128)(2,1)} %reshape.51), calls=%async_computation.2 | async-start | bytes 131072 | tf_op jit(solution)/shard_map/all_to_all | solution.py:56
  120.4 7.0 %all-to-all-done.2 = bf16[16,4,512]{2,1,0:T(4,128)(2,1)S(1)} async-done(((bf16[16,4,512]{2,1,0:T(4,128)(2,1)}), bf16[16,4,512]{2,1,0:T(4,128)(2,1)S(1)}, u32[]{:S(2)}, u32[]{:S(2)}) %all-to-all-start.2) | async-done | bytes 65568 | tf_op jit(solution)/shard_map/all_to_all | solution.py:56
  127.5 10.3 %all_to_all.48 = bf16[16,4,512]{2,1,0:T(4,128)(2,1)S(1)} all-to-all(bf16[16,4,512]{2,1,0:T(4,128)(2,1)S(1)} %broadcast_in_dim.18), channel_id=1, replica_groups=mesh['row'=32,'col_0'=8,'col_1'=2] {'col_0','col_1'}, dimensions={0} | all-to-all | bytes 131072 | tf_op jit(solution)/shard_map/all_to_all | solution.py:22
  140.3 21.4 %all_to_all.49 = f32[32,1,4096]{2,1,0:T(1,128)S(1)} all-to-all(f32[32,1,4096]{2,1,0:T(1,128)} %reshape.56), channel_id=1, replica_groups=mesh['row'=32,'col_0'=8,'col_1'=2] {'row'}, dimensions={0} | all-to-all | bytes 1048576 | tf_op jit(solution)/shard_map/all_to_all | solution.py:22
  162.1 2.8 reduce.11
  164.9 1.5 reshape.57
  166.6 5.8 %cholesky.16 = f32[64,64]{1,0:T(8,128)S(1)} custom-call(f32[64,64]{1,0:T(8,128)S(1)} %fusion.5), custom_call_target="Cholesky" | custom-call | tf_op jit(solution)/shard_map/jit(cholesky)/cholesky | solution.py:87
  173.7 4.9 %custom-call.6 = f32[1,64,64]{1,2,0:T(8,128)S(1)} custom-call(f32[1,64,64]{2,1,0:T(8,128)S(1)} %fusion.2), custom_call_target="InvertDiagBlocksLowerTriangular" | custom-call | tf_op jit(solution)/shard_map/triangular_solve | solution.py:88
  181.2 16.5 %all_to_all.50 = bf16[32,2,1024]{2,1,0:T(2,128)(2,1)S(1)} all-to-all(bf16[32,2,1024]{2,1,0:T(2,128)(2,1)S(1)} %reshape.53), channel_id=1, replica_groups=mesh['row'=32,'col_0'=8,'col_1'=2] {'row'}, dimensions={0} | all-to-all | bytes 262144 | tf_op jit(solution)/shard_map/all_to_all | solution.py:56
  197.9 14.1 %all_to_all.51 = bf16[32,2,1024]{2,1,0:T(2,128)(2,1)S(1)} all-to-all(bf16[32,2,1024]{2,1,0:T(2,128)(2,1)S(1)} %broadcast_in_dim.20), channel_id=1, replica_groups=mesh['row'=32,'col_0'=8,'col_1'=2] {'row'}, dimensions={0} | all-to-all | bytes 262144 | tf_op jit(solution)/shard_map/all_to_all | solution.py:22
  213.0 6.4 %all-to-all-start.7 = ((f32[16,1,64]{2,1,0:T(1,128)}), f32[16,1,64]{2,1,0:T(1,128)S(1)}, u32[]{:S(2)}, u32[]{:S(2)}) async-start(f32[16,1,64]{2,1,0:T(1,128)} %broadcast_in_dim.22), calls=%async_computation.7 | async-start | bytes 16384 | tf_op jit(solution)/shard_map/all_to_all | solution.py:22
  219.4 6.9 %all-to-all-done.7 = f32[16,1,64]{2,1,0:T(1,128)S(1)} async-done(((f32[16,1,64]{2,1,0:T(1,128)}), f32[16,1,64]{2,1,0:T(1,128)S(1)}, u32[]{:S(2)}, u32[]{:S(2)}) %all-to-all-start.7) | async-done | bytes 4128 | tf_op jit(solution)/shard_map/all_to_all | solution.py:22
  226.5 4.2 %subtract_convert_fusion.1 = bf16[512,1024]{1,0:T(8,128)(2,1)} fusion(bf16[512,1024]{1,0:T(8,128)(2,1)} %param.8, f32[64,512]{1,0:T(8,128)S(1)} %fusion.3, f32[64,1024]{1,0:T(8,128)S(1)} %convert_divide_fusion), kind=kOutput, calls=%fused_computation.2 | convolution fusion | flops 404750336 | bytes 2490368 | tf_op jit(solution)/shard_map/dot_general | solution.py:98
  230.8 4.2 %fusion = bf16[1024,512]{0,1:T(8,128)(2,1)} fusion(bf16[512,1024]{1,0:T(8,128)(2,1)} %subtract_convert_fusion.1, bf16[1024,1024]{1,0:T(8,128)(2,1)} %all-gather.5.cloned.1.call-done), kind=kOutput, calls=%fused_computation.4 | convolution fusion | flops 1074790400 | bytes 4194304 | tf_op jit(solution)/shard_map/dot_general | solution.py:102
  234.9 2.3 copy.22
  237.2 4.1 %all-to-all-start.8 = ((bf16[16,64,512]{2,1,0:T(8,128)(2,1)}), bf16[16,64,512]{2,1,0:T(8,128)(2,1)S(1)}, u32[]{:S(2)}, u32[]{:S(2)}) async-start(bf16[16,64,512]{2,1,0:T(8,128)(2,1)} %bitcast.33), calls=%async_computation.8 | async-start | bytes 2097152 | tf_op jit(solution)/shard_map/all_to_all | solution.py:56
  241.3 3.0 %subtract_convert_fusion = bf16[512,1024]{1,0:T(8,128)(2,1)} fusion(f32[512,1024]{1,0:T(8,128)S(1)} %multiply_add_fusion, f32[64,512]{1,0:T(8,128)S(1)} %fusion.3, bf16[64,1024]{1,0:T(8,128)(2,1)} %copy-done.1), kind=kOutput, calls=%fused_computation.1 | convolution fusion | flops 404226048 | bytes 3407872 | tf_op jit(solution)/shard_map/dot_general | solution.py:92
  244.3 25.1 %all-to-all-done.8 = bf16[16,64,512]{2,1,0:T(8,128)(2,1)S(1)} async-done(((bf16[16,64,512]{2,1,0:T(8,128)(2,1)}), bf16[16,64,512]{2,1,0:T(8,128)(2,1)S(1)}, u32[]{:S(2)}, u32[]{:S(2)}) %all-to-all-start.8) | async-done | bytes 1048608 | tf_op jit(solution)/shard_map/all_to_all | solution.py:56
  (44 shorter events, 12.4 us)
Async XLA Ops:
  7.2 98.1 %copy-start = (f32[64,1024]{1,0:T(8,128)S(1)}, f32[64,1024]{1,0:T(8,128)}, u32[]{:S(2)}) copy-start(f32[64,1024]{1,0:T(8,128)} %param.10) | copy-start | bytes 786436
  7.2 92.9 %all-gather.3.cloned.1.call-start = ((), (), s32[]{:S(2)}) async-start(), calls=%async_computation.9 | async-start | bytes 4325376 | tf_op jit(solution)/shard_map/all_gather | solution.py:75
  54.5 45.6 %copy-start.4 = (bf16[512,1024]{1,0:T(8,128)(2,1)S(1)}, bf16[512,1024]{1,0:T(8,128)(2,1)}, u32[]{:S(2)}) copy-start(bf16[512,1024]{1,0:T(8,128)(2,1)} %param.9) | copy-start | bytes 3145732
  108.1 19.4 %all-to-all-start.2 = ((bf16[16,4,512]{2,1,0:T(4,128)(2,1)}), bf16[16,4,512]{2,1,0:T(4,128)(2,1)S(1)}, u32[]{:S(2)}, u32[]{:S(2)}) async-start(bf16[16,4,512]{2,1,0:T(4,128)(2,1)} %reshape.51), calls=%async_computation.2 | async-start | bytes 131072 | tf_op jit(solution)/shard_map/all_to_all | solution.py:56
  119.7 111.1 %all-gather.5.cloned.1.call-start = ((), (), s32[]{:S(2)}) async-start(), calls=%async_computation.10 | async-start | bytes 2162688 | tf_op jit(solution)/shard_map/all_gather | solution.py:101
  137.9 0.6 copy-start.3
  213.0 13.4 %all-to-all-start.7 = ((f32[16,1,64]{2,1,0:T(1,128)}), f32[16,1,64]{2,1,0:T(1,128)S(1)}, u32[]{:S(2)}, u32[]{:S(2)}) async-start(f32[16,1,64]{2,1,0:T(1,128)} %broadcast_in_dim.22), calls=%async_computation.7 | async-start | bytes 16384 | tf_op jit(solution)/shard_map/all_to_all | solution.py:22
  219.4 15.5 %copy-start.1 = (bf16[64,1024]{1,0:T(8,128)(2,1)}, bf16[64,1024]{1,0:T(8,128)(2,1)S(1)}, u32[]{:S(2)}) copy-start(bf16[64,1024]{1,0:T(8,128)(2,1)S(1)} %reshape.54) | copy-start | bytes 393220
  226.5 8.4 %copy-start.2 = (f32[64,1024]{1,0:T(8,128)}, f32[64,1024]{1,0:T(8,128)S(1)}, u32[]{:S(2)}) copy-start(f32[64,1024]{1,0:T(8,128)S(1)} %convert_divide_fusion) | copy-start | bytes 786436
  237.2 32.2 %all-to-all-start.8 = ((bf16[16,64,512]{2,1,0:T(8,128)(2,1)}), bf16[16,64,512]{2,1,0:T(8,128)(2,1)S(1)}, u32[]{:S(2)}, u32[]{:S(2)}) async-start(bf16[16,64,512]{2,1,0:T(8,128)(2,1)} %bitcast.33), calls=%async_computation.8 | async-start | bytes 2097152 | tf_op jit(solution)/shard_map/all_to_all | solution.py:56
Sparse Core Ops, SparseCore 0:
  11.2 88.8 all-gather.2
  123.7 76.5 all-gather.4
where the time goes:
time: 278 us; the launch traced here: 277 us
  blocking collectives  108 us (39%)
  waiting for transfers between devices  84.5 us (30%)
  starting transfers between devices  22.2 us (8%)
  matrix products  21.3 us (8%)
  other arithmetic  16.2 us (6%)
  between operations  14.2 us (5%)
  local copies, waits for them, and re-layouts  10.9 us (4%)
    all_to_all x5, blocking collectives, sent_to_all(): lax.all_to_all(jnp.broadcast_to(x[None], (size, *x.shape)), axis, 0, 0, t...  91.2 us
    all_gather x1, waiting for transfers between devices, body(): act_whole = lax.all_gather(activations, 'row', axis=0, tiled=True)  44 us
    all_to_all x2, waiting for transfers between devices, sum_at_owner(): parts = lax.all_to_all(cut_along(x, dim, size), axis, 0, 0, tiled=True)  32.1 us
    all_to_all x1, blocking collectives, sum_at_owner(): parts = lax.all_to_all(cut_along(x, dim, size), axis, 0, 0, tiled=True)  16.5 us
    all_to_all x2, starting transfers between devices, sum_at_owner(): parts = lax.all_to_all(cut_along(x, dim, size), axis, 0, 0, tiled=True)  15.7 us
    all_to_all x1, waiting for transfers between devices, sent_to_all(): lax.all_to_all(jnp.broadcast_to(x[None], (size, *x.shape)), axis, 0, 0, t...  6.95 us
    another operation x3, other arithmetic, body(): factor = jnp.linalg.cholesky(gram_matrix)  6.52 us
    all_to_all x1, starting transfers between devices, sent_to_all(): lax.all_to_all(jnp.broadcast_to(x[None], (size, *x.shape)), axis, 0, 0, t...  6.39 us
  transfers between devices with their start and end apart: 5, of which 4 were waited for; matrix products, arithmetic and copies ran while one was open for 12% of the time, Pallas kernels for 0%

commit v1 on v0

v1 whole, which is shorter than its diff:
```python
import heapq
import math

import jax
import jax.numpy as jnp
from jax import lax
from jax.experimental import pallas as pl
from jax.experimental.pallas import tpu as pltpu
from jax.sharding import Mesh
from jax.sharding import PartitionSpec as P

RANK = 64
MESH = pl.DeviceIdType.MESH
momentum_decay = 0.95
learn_rate = 0.3
norm_eps = 1e-06
F32 = jnp.float32
BF16 = jnp.bfloat16
HIGHEST = lax.Precision.HIGHEST

LATENCY = 2.0
RATE = 46e3
START_NEXT = 17.0


def ring_paths(n, tie):
    reach = [d for d in range(1, (n + 1) // 2)]
    out = [d for d in reach] + [-d for d in reach]
    if n % 2 == 0:
        out.append(tie * (n // 2))
    return out


def sign(v):
    return (v > 0) - (v < 0)


def plane_tree(first, sizes):
    n1, n2 = sizes[first], sizes[1 - first]
    tree = {}

    def add(parent, child):
        tree.setdefault(parent, []).append(child)
        tree.setdefault(child, [])

    def place(d1, d2):
        return (d1, d2) if first == 0 else (d2, d1)

    tie = 1 if first == 0 else -1
    stem = sorted([0] + ring_paths(n1, tie), key=abs)
    for d1 in stem:
        if d1:
            add(place(d1 - sign(d1), 0), place(d1, 0))
    for d1 in stem:
        for d2 in sorted(ring_paths(n2, 1 if d1 % 2 else -1), key=abs):
            add(place(d1, d2 - sign(d2)), place(d1, d2))
    return tree


def planned(streams):
    free = {}
    queue = []
    order = []
    for number, stream in enumerate(streams):
        heapq.heappush(queue, (stream["start"], 0, number, stream["root"]))
    while queue:
        now, kind, number, spot = heapq.heappop(queue)
        stream = streams[number]
        order.append((now, number, spot))
        for child in stream["tree"][spot]:
            link = stream["link"](spot, child)
            rate = RATE if link != "pair" else 5e5
            begin = max(now, free.get(link, 0.0))
            free[link] = begin + stream["bytes"] / rate
            heapq.heappush(queue, (free[link] + LATENCY, 1, number, child))
    return order


def split2(v):
    hi = v.astype(BF16)
    return hi, (v - hi.astype(F32)).astype(BF16)


def split3(v):
    hi = v.astype(BF16)
    rest = v - hi.astype(F32)
    mid = rest.astype(BF16)
    return hi, mid, (rest - mid.astype(F32)).astype(BF16)


def dot_nn(a, b, precision=None):
    return lax.dot_general(a, b, (((1,), (0,)), ((), ())), preferred_element_type=F32, precision=precision)


def dot_nt(a, b, precision=None):
    return lax.dot_general(a, b, (((1,), (1,)), ((), ())), preferred_element_type=F32, precision=precision)


def dot_tn(a, b, precision=None):
    return lax.dot_general(a, b, (((0,), (0,)), ((), ())), preferred_element_type=F32, precision=precision)


def build(mesh, shapes):
    nx, ny, nz, nc = (mesh.shape[a] for a in ("x", "y", "z", "c"))
    plane, cols = nx * ny, nz * nc
    t_act, width = shapes["act"]
    t_cot, rows = shapes["cot"]
    n_next = shapes["nxt"][0]
    tokens = t_act * plane
    n_out = n_next * plane // cols
    half = n_out // 2
    d_out, d_in = rows * plane, width * cols
    grad_scale = 1.0 / math.sqrt(tokens)
    out_scale = 1.0 / math.sqrt(d_in)
    step_scale = learn_rate * math.sqrt(d_out * d_in / RANK)
    feed_scale = 1.0 - momentum_decay
    wy = width * 5 // 8
    wx = width - wy
    rpc = RANK // cols
    r_groups = RANK // 16
    c_groups = plane // r_groups
    c_width = width // c_groups

    tree_y, tree_x = plane_tree(1, (nx, ny)), plane_tree(0, (nx, ny))

    def plane_link(a, b):
        return ("x", b[0] - a[0]) if a[1] == b[1] else ("y", b[1] - a[1])

    def cot_tree():
        tree = {}
        for d in sorted([0] + ring_paths(nz, 1), key=abs):
            if d:
                tree[(d - sign(d), 0)].append((d, 0))
            tree[(d, 0)] = [(d, 1)] if nc > 1 else []
            if nc > 1:
                tree[(d, 1)] = []
        return tree

    def cot_link(a, b):
        return "pair" if a[1] != b[1] else ("z", b[0] - a[0])

    streams = [
        dict(tree=tree_y, bytes=t_act * wy * 2, start=0.0, root=(0, 0), link=plane_link, kind="plane"),
        dict(tree=tree_x, bytes=t_act * wx * 2, start=0.0, root=(0, 0), link=plane_link, kind="plane"),
        dict(tree=cot_tree(), bytes=t_cot * rows * 2, start=0.0, root=(0, 0), link=cot_link, kind="col"),
        dict(tree=tree_y, bytes=n_next * wy * 2, start=START_NEXT, root=(0, 0), link=plane_link, kind="plane"),
        dict(tree=tree_x, bytes=n_next * wx * 2, start=START_NEXT, root=(0, 0), link=plane_link, kind="plane"),
    ]
    order = planned(streams)
    ids = {}
    for _, number, spot in order:
        if spot != (0, 0):
            ids[(number, spot)] = len(ids)
    n_bulk = len(ids)

    def kernel(
        act, cot, w_in, m_in, rb, nxt,
        w_out, m_out, b_out, o_out,
        a_y, a_x, c_all, n_y, n_x, c_t, w, m, v,
        buf, b_hi, b_lo,
        u_s, u_r, v_s, v_r, u_m, u_g, u_full, l_s, l_g, left, g_s, g_r, g_m, g_g, gram,
        orth, r_s, r_r, r_m, r_g, rmat,
        p_s, p_r, q_s, q_r, y_s, y_r, s_s, s_r,
        bulk_send, bulk_recv, small_send, small_recv, local_sem,
    ):
        x, y, z, c = (lax.axis_index(a) for a in ("x", "y", "z", "c"))
        me_row, me_col = x * ny + y, z * nc + c
        stores = [a_y, a_x, c_all, n_y, n_x]

        def local(src, dst, k):
            return pltpu.make_async_copy(src, dst, local_sem.at[k])

        ky, kx = pl.ds(0, wy), pl.ds(wy, wx)
        loads = [
            local(act.at[:, ky], a_y.at[me_row], 0),
            local(act.at[:, kx], a_x.at[me_row], 1),
            local(cot, c_all.at[me_col], 2),
            local(rb, v, 3),
            local(m_in, m, 4),
            local(nxt.at[:, ky], n_y.at[me_row], 5),
            local(nxt.at[:, kx], n_x.at[me_row], 6),
            local(w_in, w, 7),
        ]
        for copy in loads:
            copy.start()

        def plane_peer(k):
            return (x + k // ny) % nx, (y + k % ny) % ny

        def col_peer(k):
            return (z + k // nc) % nz, (c + k % nc) % nc

        barrier = pltpu.get_barrier_semaphore()

        def greet_plane(k, carry):
            px, py = plane_peer(k)
            pl.semaphore_signal(barrier, inc=1, device_id={"x": px, "y": py}, device_id_type=MESH)
            return carry

        def greet_col(k, carry):
            pz, pc = col_peer(k)
            pl.semaphore_signal(barrier, inc=1, device_id={"z": pz, "c": pc}, device_id_type=MESH)
            return carry

        lax.fori_loop(1, plane, greet_plane, 0)
        lax.fori_loop(1, cols, greet_col, 0)
        pl.semaphore_wait(barrier, plane - 1 + cols - 1)

        def origin_slot(number, spot):
            if streams[number]["kind"] == "plane":
                return ((x - spot[0]) % nx) * ny + (y - spot[1]) % ny
            return ((z - spot[0]) % nz) * nc + (c - spot[1]) % nc

        def hop(number, spot, child):
            if streams[number]["kind"] == "plane":
                return {"x": (x + child[0] - spot[0]) % nx, "y": (y + child[1] - spot[1]) % ny}
            return {"z": (z + child[0] - spot[0]) % nz, "c": (c + child[1] - spot[1]) % nc}

        def bulk(number, spot, child):
            ref = stores[number].at[origin_slot(number, spot)]
            k = ids[(number, child)]
            return pltpu.make_async_remote_copy(
                src_ref=ref,
                dst_ref=ref,
                send_sem=bulk_send.at[k],
                recv_sem=bulk_recv.at[k],
                device_id=hop(number, spot, child),
                device_id_type=MESH,
            )

        sent = []
        pending = list(order)

        def take(number, spot):
            if spot == (0, 0):
                if number < 3:
                    loads[number].wait()
                else:
                    loads[number + 2].wait()
            else:
                ref = stores[number].at[origin_slot(number, spot)]
                k = ids[(number, spot)]
                pltpu.make_async_copy(ref, ref, bulk_recv.at[k]).wait()
            for child in streams[number]["tree"][spot]:
                copy = bulk(number, spot, child)
                copy.start()
                sent.append(copy)
            if number == 2:
                slot = origin_slot(number, spot)
                piece = c_all[slot]
                at = pl.multiple_of(slot * t_cot, t_cot)
                c_t[:, pl.ds(at, t_cot)] = piece.T

        def advance(until):
            while pending and pending[0][0] <= until:
                _, number, spot = pending.pop(0)
                take(number, spot)

        def finish(numbers):
            while any(p[1] in numbers for p in pending):
                _, number, spot = pending.pop(0)
                take(number, spot)

        drains = []

        def exchange(k_sem, source, dest, group):
            count = plane if group == "plane" else cols
            mine = me_row if group == "plane" else me_col

            def one(k, carry):
                if group == "plane":
                    px, py = plane_peer(k)
                    where, slot = {"x": px, "y": py}, px * ny + py
                else:
                    pz, pc = col_peer(k)
                    where, slot = {"z": pz, "c": pc}, pz * nc + pc
                pltpu.make_async_remote_copy(
                    src_ref=source(slot),
                    dst_ref=dest.at[mine],
                    send_sem=small_send.at[k_sem],
                    recv_sem=small_recv.at[k_sem],
                    device_id=where,
                    device_id_type=MESH,
                ).start()
                return carry

            lax.fori_loop(1, count, one, 0)
            part = dest.at[pl.ds(0, count - 1)]
            drains.append(pltpu.make_async_copy(part, part, small_send.at[k_sem]))
            return pltpu.make_async_copy(part, part, small_recv.at[k_sem])

        advance(0.0)

        loads[3].wait()
        v3 = jnp.concatenate(split3(v[...]), axis=0)

        def fold3(t):
            return t[:RANK] + t[RANK : 2 * RANK] + t[2 * RANK :]

        lane = lax.broadcasted_iota(jnp.int32, (RANK, 2 * t_act), 1)
        here = (lane // t_act) == (me_row % 2)
        own_y, own_x = a_y[me_row], a_x[me_row]
        u_part = fold3(
            dot_nt(v3[:, :wy], jnp.concatenate([own_y, own_y], axis=0))
            + dot_nt(v3[:, wy:], jnp.concatenate([own_x, own_x], axis=0))
        )
        u_part = jnp.where(here, u_part, 0.0)
        for k in range(cols):
            u_s[k] = u_part[k * rpc : (k + 1) * rpc]
        u_r[me_col] = u_s[me_col]
        wait_u = exchange(0, lambda s: u_s.at[s], u_r, "col")
        loads[4].wait()
        v_part = fold3(dot_nt(v3, m[...]))
        for k in range(cols):
            v_s[k] = v_part[k * rpc : (k + 1) * rpc]
        v_r[me_col] = v_s[me_col]
        wait_v = exchange(1, lambda s: v_s.at[s], v_r, "col")
        advance(6.0)
        wait_u.wait()
        u_m[...] = jnp.sum(u_r[...], axis=0)
        u_g[me_row] = u_m[...]
        wait_ug = exchange(2, lambda s: u_m, u_g, "plane")
        advance(14.0)
        finish((2,))
        wait_ug.wait()
        u_full[...] = jnp.zeros_like(u_full)
        for k in range(plane // 2):
            u_full[0:rpc, k * 2 * t_act : (k + 1) * 2 * t_act] = u_g[2 * k] + u_g[2 * k + 1]
        u_rows = u_full.shape[0]
        u3 = jnp.concatenate([t.astype(F32) for t in split3(u_full[...])], axis=0).astype(BF16)
        from_gradient = dot_nt(u3, c_t[...])
        from_gradient = from_gradient[:u_rows] + from_gradient[u_rows : 2 * u_rows] + from_gradient[2 * u_rows :]
        wait_v.wait()
        l_s[...] = jnp.sum(v_r[...], axis=0) + grad_scale * from_gradient[:rpc]
        l_g[me_col] = l_s[...]
        wait_l = exchange(3, lambda s: l_s, l_g, "col")
        advance(20.0)
        wait_l.wait()
        for k in range(cols):
            left[k * rpc : (k + 1) * rpc, :] = l_g[k]
        whole_left = left[...]
        u_full[0:rpc, 0:rows] = l_s[...]
        g_part = dot_nt(u_full[:, 0:rows], whole_left, HIGHEST)
        g_s[...] = jnp.concatenate([g_part[:rpc], jnp.zeros((rpc, 128 - RANK), F32)], axis=1)
        g_r[me_row] = g_s[...]
        wait_g = exchange(4, lambda s: g_s, g_r, "plane")

        finish((0, 1))
        gathered_y = a_y[...].reshape(tokens, wy)
        gathered_x = a_x[...].reshape(tokens, wx)
        block = min(128, rows)

        def gradient_block(i, carry):
            at = pl.ds(pl.multiple_of(i * block, block), block)
            lhs = c_t[at, :]
            for cut, gathered in ((ky, gathered_y), (kx, gathered_x)):
                value = m[at, cut].astype(F32) + grad_scale * dot_nn(lhs, gathered)
                buf[at, cut] = value
                hi, lo = split2(value)
                b_hi[at, cut] = hi
                b_lo[at, cut] = lo
            return carry

        lax.fori_loop(0, rows // block, gradient_block, 0)
        wait_g.wait()
        g_m[...] = jnp.sum(g_r[...], axis=0)
        g_g[me_col] = g_m[...]
        wait_gg = exchange(5, lambda s: g_m, g_g, "col")
        advance(32.0)
        wait_gg.wait()
        for k in range(cols):
            gram[k * rpc : (k + 1) * rpc, :] = g_g[k]

        sub = lax.broadcasted_iota(jnp.int32, (RANK, 128), 0)
        lan = lax.broadcasted_iota(jnp.int32, (RANK, 128), 1)
        aug = jnp.where(lan - RANK == sub, 1.0, gram[...])
        for j in range(RANK - 1):
            row = aug[j : j + 1, :]
            col = aug[:, j : j + 1] / aug[j : j + 1, j : j + 1]
            aug = aug - jnp.where(sub > j, col * row, 0.0)
        pivot = jnp.sum(jnp.where(lan == sub, aug, 0.0), axis=1, keepdims=True)
        inverse = aug[:, RANK:] / jnp.sqrt(pivot)
        orth[...] = dot_nn(inverse, whole_left, HIGHEST)

        o_hi, o_lo = split2(orth[...])
        o_both = jnp.concatenate([o_hi, o_lo], axis=0)
        with_hi = dot_nn(o_both, b_hi[...])
        r_part = (with_hi[:RANK] + with_hi[RANK:]) + dot_nn(o_hi, b_lo[...])
        r_part = r_part.astype(BF16)
        for i in range(r_groups):
            for j in range(c_groups):
                r_s[i * c_groups + j] = r_part[16 * i : 16 * i + 16, j * c_width : (j + 1) * c_width]
        r_r[me_row] = r_s[me_row]
        wait_r = exchange(6, lambda s: r_s.at[s], r_r, "plane")
        finish((3, 4))

        loads[7].wait()
        per = n_out // n_next

        def product_block(i, carry):
            at = pl.ds(i * per, per)
            value = dot_nt(n_y[at].reshape(n_out, wy), w[:, :wy]) + dot_nt(n_x[at].reshape(n_out, wx), w[:, wy:])
            p_s[i % nc, i // nc] = (value * out_scale).astype(BF16)
            return carry

        lax.fori_loop(0, cols, product_block, 0)
        to_pair = pltpu.make_async_remote_copy(
            src_ref=p_s.at[1 - c],
            dst_ref=p_r,
            send_sem=small_send.at[7],
            recv_sem=small_recv.at[7],
            device_id={"c": 1 - c},
            device_id_type=MESH,
        )
        to_pair.start()
        wait_r.wait()
        r_m[...] = jnp.sum(r_r[...].astype(F32), axis=0).astype(BF16)
        r_g[me_row] = r_m[...]
        wait_rg = exchange(8, lambda s: r_m, r_g, "plane")
        to_pair.wait_recv()
        for k in range(nz):
            q_s[k] = (p_s[c, k].astype(F32) + p_r[k].astype(F32)).astype(BF16)

        def send_q(k, carry):
            pz = (z + k) % nz
            pltpu.make_async_remote_copy(
                src_ref=q_s.at[pz],
                dst_ref=q_r.at[z],
                send_sem=small_send.at[9],
                recv_sem=small_recv.at[9],
                device_id={"z": pz},
                device_id_type=MESH,
            ).start()
            return carry

        q_r[z] = q_s[z]
        lax.fori_loop(1, nz, send_q, 0)
        q_part = q_r.at[pl.ds(0, nz - 1)]
        wait_q = pltpu.make_async_copy(q_part, q_part, small_recv.at[9])
        drains.append(pltpu.make_async_copy(q_part, q_part, small_send.at[9]))
        wait_rg.wait()
        for i in range(r_groups):
            for j in range(c_groups):
                rmat[16 * i : 16 * i + 16, j * c_width : (j + 1) * c_width] = r_g[i * c_groups + j]
        right = rmat[...]
        right_f = right.astype(F32)
        squares = dot_nt(jnp.ones((8, width), F32), right_f * right_f, HIGHEST)
        s_s[...] = jnp.concatenate([squares, squares], axis=1)
        s_r[me_col] = s_s[...]
        wait_s = exchange(10, lambda s: s_s, s_r, "col")
        y_part = dot_nt(n_y[...].reshape(n_next * plane, wy), right[:, :wy])
        y_part = y_part + dot_nt(n_x[...].reshape(n_next * plane, wx), right[:, wy:])
        for k in range(cols):
            at = k * n_out
            y_s[k] = jnp.concatenate([y_part[at : at + half], y_part[at + half : at + n_out]], axis=1).astype(BF16)
        y_r[me_col] = y_s[me_col]
        wait_y = exchange(11, lambda s: y_s.at[s], y_r, "col")

        both = jnp.concatenate([right, right], axis=0)


        feed = dot_tn(o_both, both)
        m_out[...] = (buf[...] - feed_scale * feed).astype(BF16)

        wait_s.wait()
        total = jnp.sum(s_r[...], axis=0)[0:1]
        total = jnp.sum(jnp.where(lan == sub, total, 0.0), axis=1, keepdims=True)
        scale = 1.0 / jnp.sqrt(total + norm_eps)
        b_out[...] = right_f * scale
        scaled = orth[...] * (scale * step_scale)
        s_both = jnp.concatenate(split2(scaled), axis=0)
        w_out[...] = (w[...].astype(F32) - dot_tn(s_both, both)).astype(BF16)
        wait_y.wait()
        y_sum = jnp.sum(y_r[...].astype(F32), axis=0)
        y_sum = jnp.concatenate([y_sum[:, :RANK], y_sum[:, RANK:]], axis=0)
        low = dot_nn(y_sum * out_scale, scaled, HIGHEST)
        wait_q.wait()
        o_out[...] = (jnp.sum(q_r[...].astype(F32), axis=0) - low).astype(BF16)

        for copy in sent:
            copy.wait_send()
        to_pair.wait_send()
        for copy in drains:
            copy.wait()

    sub8 = max(8, rpc)
    vmem = pltpu.VMEM
    scratch = [
        vmem((plane, t_act, wy), BF16),
        vmem((plane, t_act, wx), BF16),
        vmem((cols, t_cot, rows), BF16),
        vmem((plane, n_next, wy), BF16),
        vmem((plane, n_next, wx), BF16),
        vmem((rows, tokens), BF16),
        vmem((rows, width), BF16),
        vmem((rows, width), BF16),
        vmem((RANK, width), F32),
        vmem((rows, width), F32),
        vmem((rows, width), BF16),
        vmem((rows, width), BF16),
        vmem((cols, rpc, 128), F32),
        vmem((cols, rpc, 128), F32),
        vmem((cols, rpc, rows), F32),
        vmem((cols, rpc, rows), F32),
        vmem((rpc, 128), F32),
        vmem((plane, rpc, 128), F32),
        vmem((sub8, tokens), F32),
        vmem((rpc, rows), F32),
        vmem((cols, rpc, rows), F32),
        vmem((RANK, rows), F32),
        vmem((rpc, 128), F32),
        vmem((plane, rpc, 128), F32),
        vmem((rpc, 128), F32),
        vmem((cols, rpc, 128), F32),
        vmem((RANK, 128), F32),
        vmem((RANK, rows), F32),
        vmem((plane, 16, c_width), BF16),
        vmem((plane, 16, c_width), BF16),
        vmem((16, c_width), BF16),
        vmem((plane, 16, c_width), BF16),
        vmem((RANK, width), BF16),
        vmem((nc, nz, n_out, rows), BF16),
        vmem((nz, n_out, rows), BF16),
        vmem((nz, n_out, rows), BF16),
        vmem((nz, n_out, rows), BF16),
        vmem((cols, half, 128), BF16),
        vmem((cols, half, 128), BF16),
        vmem((8, 128), F32),
        vmem((cols, 8, 128), F32),
        pltpu.SemaphoreType.DMA((n_bulk,)),
        pltpu.SemaphoreType.DMA((n_bulk,)),
        pltpu.SemaphoreType.DMA((12,)),
        pltpu.SemaphoreType.DMA((12,)),
        pltpu.SemaphoreType.DMA((8,)),
    ]
    return pl.pallas_call(
        kernel,
        out_shape=(
            jax.ShapeDtypeStruct((rows, width), BF16),
            jax.ShapeDtypeStruct((rows, width), BF16),
            jax.ShapeDtypeStruct((RANK, width), F32),
            jax.ShapeDtypeStruct((n_out, rows), BF16),
        ),
        in_specs=[pl.BlockSpec(memory_space=pl.ANY)] * 6,
        out_specs=[pl.BlockSpec(memory_space=pltpu.VMEM)] * 4,
        scratch_shapes=scratch,
        compiler_params=pltpu.CompilerParams(
            collective_id=0, has_side_effects=True, vmem_limit_bytes=60 * 1024 * 1024
        ),
    )


def solution(mesh, sizes=(4, 8, 8, 2)):
    torus = Mesh(mesh.devices.reshape(sizes), ("x", "y", "z", "c"))
    row, col = ("x", "y"), ("z", "c")

    def body(activations, cotangents, weights, momentum, right_basis, next_inputs):
        shapes = dict(act=activations.shape, cot=cotangents.shape, nxt=next_inputs.shape)
        return build(torus, shapes)(activations, cotangents, weights, momentum, right_basis, next_inputs)

    return jax.shard_map(
        body,
        mesh=torus,
        in_specs=(P(row, col), P(col, row), P(row, col), P(row, col), P(None, col), P(row, col)),
        out_specs=(P(row, col), P(row, col), P(None, col), P(col, row)),
        check_vma=False,
    )
```

time: 278 us -> 120 us (0.43)
  Pallas kernels: 0 us -> 114 us
  blocking collectives: 108 us -> 0 us
  waiting for transfers between devices: 84.5 us -> 0 us
  starting transfers between devices: 22.2 us -> 0 us
  matrix products: 21.3 us -> 0 us
  other arithmetic: 16.2 us -> 0 us
  between operations: 14.2 us -> 0.65 us
  local copies, waits for them, and re-layouts: 10.9 us -> 4.94 us
    pallas_call x0 -> x1, Pallas kernels: none -> 114 us  [body(): build(torus, shapes)]
    all_to_all x6 -> x0, blocking collectives: 108 us -> none  [the longest x5 91.2 us: sent_to_all(): lax.all_to_all(jnp.broadcast_to(x[None], (size, *x.shape)), axis, 0, 0, t...]
    all_gather x2 -> x0, waiting for transfers between devices: 44.1 us -> none  [the longest x1 44 us: body(): act_whole = lax.all_gather(activations, 'row', axis=0, tiled=True)]
    all_to_all x3 -> x0, waiting for transfers between devices: 39 us -> none  [the longest x2 32.1 us: sum_at_owner(): parts = lax.all_to_all(cut_along(x, dim, size), axis, 0, 0, tiled=True)]
    all_to_all x3 -> x0, starting transfers between devices: 22.1 us -> none  [the longest x2 15.7 us: sum_at_owner(): parts = lax.all_to_all(cut_along(x, dim, size), axis, 0, 0, tiled=True)]
    dot_general x7 -> x0, matrix products: 20.2 us -> none  [the longest x1 5.17 us: body(): lax.dot_general(gathered_by_axis(cotangents, ('col_0', 'col_1'), 0), act_...]
    another operation x5 -> x0, other arithmetic: 12.1 us -> none  [the longest x3 6.52 us: body(): factor = jnp.linalg.cholesky(gram_matrix)]
  transfers between devices with their start and end apart: 5 -> 0, of which waited for: 4 -> 0; matrix products, arithmetic and copies ran while one was open for 12% -> 0% of each run, Pallas kernels for 0% -> 0%
where the time goes in v1:
time: 120 us
  Pallas kernels  114 us (95%)
  local copies, waits for them, and re-layouts  4.94 us (4%)
    pallas_call x1, Pallas kernels, body(): build(torus, shapes)  114 us
    unnamed x10, local copies, waits for them, and re-layouts  4.94 us

profile of v1, /device:TPU:1, one launch (start us, length us, event | category | flops | bytes accessed | tf_op | source)
XLA Modules:
  0.0 120.0 jit_solution(15290724257614228997)
XLA Ops:
  0.6 114.4 %shard_map.93 = (bf16[512,1024]{1,0:T(8,128)(2,1)}, bf16[512,1024]{1,0:T(8,128)(2,1)}, f32[64,1024]{1,0:T(8,128)}, bf16[64,512]{1,0:T(8,128)(2,1)}) custom-call(bf16[64,1024]{1,0:T(8,128)(2,1)} %act.1, bf16[128,512]{1,0:T(8,128)(2,1)} %cot.1, bf16[512,1024]{1,0:T(8,128)(2,1)} %w_in.1, bf16[512,1024]{1,0:T(8,128)(2,1)} %m_in.1, f32[64,1024]{1,0:T(8,128)} %rb.1, ...), custom_call_target="tpu_custom_call" | custom-call | tf_op jit(solution)/shard_map/pallas_call | solution.py:559
  115.1 0.0 copy-start
  115.1 2.4 %copy.14 = bf16[512,1024]{1,0:T(8,128)(2,1)} copy(bf16[512,1024]{1,0:T(8,128)(2,1)} %get-tuple-element.8) | data formatting | bytes 2097152
  117.4 0.0 copy-done
  117.4 0.0 copy-start.1
  117.4 1.0 copy.15
  118.4 0.1 copy-done.1
  118.5 0.0 copy-start.2
  118.5 0.7 copy.16
  119.2 0.2 copy-done.2
  119.4 0.6 copy.17
Async XLA Ops:
  115.1 2.4 %copy-start = (bf16[512,1024]{1,0:T(8,128)(2,1)S(1)}, bf16[512,1024]{1,0:T(8,128)(2,1)}, u32[]{:S(2)}) copy-start(bf16[512,1024]{1,0:T(8,128)(2,1)} %get-tuple-element.9) | copy-start | bytes 3145732
  117.4 1.1 copy-start.1
  118.5 0.9 copy-start.2

commit v2 on v1

--- a/solution.py
+++ b/solution.py
@@ -18,9 +18,11 @@
 BF16 = jnp.bfloat16
 HIGHEST = lax.Precision.HIGHEST
 
-LATENCY = 2.0
-RATE = 46e3
-START_NEXT = 17.0
+LATENCY = 2.5
+RATE = 36e3
+START_NEXT = 0.0
+START_ACT = 8.0
+T = (5.0, 13.0, 21.0, 26.0, 32.0, 38.0, 45.0, 53.0, 61.0)
 
 
 def ring_paths(n, tie):
@@ -62,17 +64,22 @@
     queue = []
     order = []
     for number, stream in enumerate(streams):
-        heapq.heappush(queue, (stream["start"], 0, number, stream["root"]))
+        heapq.heappush(queue, (stream["start"], len(queue), False, number, stream["root"], None))
+    count = len(queue)
     while queue:
-        now, kind, number, spot = heapq.heappop(queue)
+        now, _, is_send, number, spot, child = heapq.heappop(queue)
+        order.append((now, is_send, number, spot, child))
+        if is_send:
+            continue
         stream = streams[number]
-        order.append((now, number, spot))
         for child in stream["tree"][spot]:
             link = stream["link"](spot, child)
-            rate = RATE if link != "pair" else 5e5
+            cost = stream["bytes"] / (RATE if link != "pair" else 5e5)
             begin = max(now, free.get(link, 0.0))
-            free[link] = begin + stream["bytes"] / rate
-            heapq.heappush(queue, (free[link] + LATENCY, 1, number, child))
+            free[link] = begin + cost
+            heapq.heappush(queue, (max(now, begin - cost), count, True, number, spot, child))
+            heapq.heappush(queue, (free[link] + LATENCY, count + 1, False, number, child, None))
+            count += 2
     return order
 
 
@@ -140,16 +147,16 @@
         return "pair" if a[1] != b[1] else ("z", b[0] - a[0])
 
     streams = [
-        dict(tree=tree_y, bytes=t_act * wy * 2, start=0.0, root=(0, 0), link=plane_link, kind="plane"),
-        dict(tree=tree_x, bytes=t_act * wx * 2, start=0.0, root=(0, 0), link=plane_link, kind="plane"),
+        dict(tree=tree_y, bytes=t_act * wy * 2, start=START_ACT, root=(0, 0), link=plane_link, kind="plane"),
+        dict(tree=tree_x, bytes=t_act * wx * 2, start=START_ACT, root=(0, 0), link=plane_link, kind="plane"),
         dict(tree=cot_tree(), bytes=t_cot * rows * 2, start=0.0, root=(0, 0), link=cot_link, kind="col"),
         dict(tree=tree_y, bytes=n_next * wy * 2, start=START_NEXT, root=(0, 0), link=plane_link, kind="plane"),
         dict(tree=tree_x, bytes=n_next * wx * 2, start=START_NEXT, root=(0, 0), link=plane_link, kind="plane"),
     ]
     order = planned(streams)
     ids = {}
-    for _, number, spot in order:
-        if spot != (0, 0):
+    for _, is_send, number, spot, _ in order:
+        if not is_send and spot != (0, 0):
             ids[(number, spot)] = len(ids)
     n_bulk = len(ids)
 
@@ -157,7 +164,7 @@
         act, cot, w_in, m_in, rb, nxt,
         w_out, m_out, b_out, o_out,
         a_y, a_x, c_all, n_y, n_x, c_t, w, m, v,
-        buf, b_hi, b_lo,
+        s_m, l_pad, o_both,
         u_s, u_r, v_s, v_r, u_m, u_g, u_full, l_s, l_g, left, g_s, g_r, g_m, g_g, gram,
         orth, r_s, r_r, r_m, r_g, rmat,
         p_s, p_r, q_s, q_r, y_s, y_r, s_s, s_r,
@@ -204,8 +211,6 @@
 
         lax.fori_loop(1, plane, greet_plane, 0)
         lax.fori_loop(1, cols, greet_col, 0)
-        pl.semaphore_wait(barrier, plane - 1 + cols - 1)
-
         def origin_slot(number, spot):
             if streams[number]["kind"] == "plane":
                 return ((x - spot[0]) % nx) * ny + (y - spot[1]) % ny
@@ -231,35 +236,26 @@
         sent = []
         pending = list(order)
 
-        def take(number, spot):
-            if spot == (0, 0):
-                if number < 3:
-                    loads[number].wait()
-                else:
-                    loads[number + 2].wait()
-            else:
-                ref = stores[number].at[origin_slot(number, spot)]
-                k = ids[(number, spot)]
-                pltpu.make_async_copy(ref, ref, bulk_recv.at[k]).wait()
-            for child in streams[number]["tree"][spot]:
+        def step():
+            _, is_send, number, spot, child = pending.pop(0)
+            if is_send:
                 copy = bulk(number, spot, child)
                 copy.start()
                 sent.append(copy)
-            if number == 2:
-                slot = origin_slot(number, spot)
-                piece = c_all[slot]
-                at = pl.multiple_of(slot * t_cot, t_cot)
-                c_t[:, pl.ds(at, t_cot)] = piece.T
+            elif spot == (0, 0):
+                if number >= 2:
+                    loads[number if number == 2 else number + 2].wait()
+            else:
+                ref = stores[number].at[origin_slot(number, spot)]
+                pltpu.make_async_copy(ref, ref, bulk_recv.at[ids[(number, spot)]]).wait()
 
         def advance(until):
             while pending and pending[0][0] <= until:
-                _, number, spot = pending.pop(0)
-                take(number, spot)
+                step()
 
         def finish(numbers):
-            while any(p[1] in numbers for p in pending):
-                _, number, spot = pending.pop(0)
-                take(number, spot)
+            while any(p[2] in numbers for p in pending):
+                step()
 
         drains = []
 
@@ -289,8 +285,6 @@
             drains.append(pltpu.make_async_copy(part, part, small_send.at[k_sem]))
             return pltpu.make_async_copy(part, part, small_recv.at[k_sem])
 
-        advance(0.0)
-
         loads[3].wait()
         v3 = jnp.concatenate(split3(v[...]), axis=0)
 
@@ -299,6 +293,8 @@
 
         lane = lax.broadcasted_iota(jnp.int32, (RANK, 2 * t_act), 1)
         here = (lane // t_act) == (me_row % 2)
+        loads[0].wait()
+        loads[1].wait()
         own_y, own_x = a_y[me_row], a_x[me_row]
         u_part = fold3(
             dot_nt(v3[:, :wy], jnp.concatenate([own_y, own_y], axis=0))
@@ -308,90 +304,57 @@
         for k in range(cols):
             u_s[k] = u_part[k * rpc : (k + 1) * rpc]
         u_r[me_col] = u_s[me_col]
+        pl.semaphore_wait(barrier, plane - 1 + cols - 1)
         wait_u = exchange(0, lambda s: u_s.at[s], u_r, "col")
+        advance(0.0)
         loads[4].wait()
         v_part = fold3(dot_nt(v3, m[...]))
         for k in range(cols):
             v_s[k] = v_part[k * rpc : (k + 1) * rpc]
         v_r[me_col] = v_s[me_col]
         wait_v = exchange(1, lambda s: v_s.at[s], v_r, "col")
-        advance(6.0)
+        advance(T[0])
         wait_u.wait()
         u_m[...] = jnp.sum(u_r[...], axis=0)
         u_g[me_row] = u_m[...]
         wait_ug = exchange(2, lambda s: u_m, u_g, "plane")
-        advance(14.0)
+        advance(T[1])
         finish((2,))
         wait_ug.wait()
         u_full[...] = jnp.zeros_like(u_full)
         for k in range(plane // 2):
             u_full[0:rpc, k * 2 * t_act : (k + 1) * 2 * t_act] = u_g[2 * k] + u_g[2 * k + 1]
-        u_rows = u_full.shape[0]
-        u3 = jnp.concatenate([t.astype(F32) for t in split3(u_full[...])], axis=0).astype(BF16)
-        from_gradient = dot_nt(u3, c_t[...])
-        from_gradient = from_gradient[:u_rows] + from_gradient[u_rows : 2 * u_rows] + from_gradient[2 * u_rows :]
+        n8 = u_full.shape[0]
+
+        def stacked(value):
+            return jnp.concatenate([t.astype(F32) for t in split3(value)], axis=0).astype(BF16)
+
+        def unstacked(t):
+            return t[:n8] + t[n8 : 2 * n8] + t[2 * n8 :]
+
+        cot_rows = c_all[...].reshape(tokens, rows)
+        from_gradient = unstacked(dot_nn(stacked(u_full[...]), cot_rows))
         wait_v.wait()
         l_s[...] = jnp.sum(v_r[...], axis=0) + grad_scale * from_gradient[:rpc]
         l_g[me_col] = l_s[...]
         wait_l = exchange(3, lambda s: l_s, l_g, "col")
-        advance(20.0)
+        advance(T[2])
         wait_l.wait()
         for k in range(cols):
             left[k * rpc : (k + 1) * rpc, :] = l_g[k]
         whole_left = left[...]
-        u_full[0:rpc, 0:rows] = l_s[...]
-        g_part = dot_nt(u_full[:, 0:rows], whole_left, HIGHEST)
-        g_s[...] = jnp.concatenate([g_part[:rpc], jnp.zeros((rpc, 128 - RANK), F32)], axis=1)
-        g_r[me_row] = g_s[...]
-        wait_g = exchange(4, lambda s: g_s, g_r, "plane")
-
-        finish((0, 1))
-        gathered_y = a_y[...].reshape(tokens, wy)
-        gathered_x = a_x[...].reshape(tokens, wx)
-        block = min(128, rows)
-
-        def gradient_block(i, carry):
-            at = pl.ds(pl.multiple_of(i * block, block), block)
-            lhs = c_t[at, :]
-            for cut, gathered in ((ky, gathered_y), (kx, gathered_x)):
-                value = m[at, cut].astype(F32) + grad_scale * dot_nn(lhs, gathered)
-                buf[at, cut] = value
-                hi, lo = split2(value)
-                b_hi[at, cut] = hi
-                b_lo[at, cut] = lo
-            return carry
-
-        lax.fori_loop(0, rows // block, gradient_block, 0)
-        wait_g.wait()
-        g_m[...] = jnp.sum(g_r[...], axis=0)
-        g_g[me_col] = g_m[...]
-        wait_gg = exchange(5, lambda s: g_m, g_g, "col")
-        advance(32.0)
-        wait_gg.wait()
-        for k in range(cols):
-            gram[k * rpc : (k + 1) * rpc, :] = g_g[k]
-
-        sub = lax.broadcasted_iota(jnp.int32, (RANK, 128), 0)
-        lan = lax.broadcasted_iota(jnp.int32, (RANK, 128), 1)
-        aug = jnp.where(lan - RANK == sub, 1.0, gram[...])
-        for j in range(RANK - 1):
-            row = aug[j : j + 1, :]
-            col = aug[:, j : j + 1] / aug[j : j + 1, j : j + 1]
-            aug = aug - jnp.where(sub > j, col * row, 0.0)
-        pivot = jnp.sum(jnp.where(lan == sub, aug, 0.0), axis=1, keepdims=True)
-        inverse = aug[:, RANK:] / jnp.sqrt(pivot)
-        orth[...] = dot_nn(inverse, whole_left, HIGHEST)
-
-        o_hi, o_lo = split2(orth[...])
-        o_both = jnp.concatenate([o_hi, o_lo], axis=0)
-        with_hi = dot_nn(o_both, b_hi[...])
-        r_part = (with_hi[:RANK] + with_hi[RANK:]) + dot_nn(o_hi, b_lo[...])
-        r_part = r_part.astype(BF16)
-        for i in range(r_groups):
-            for j in range(c_groups):
-                r_s[i * c_groups + j] = r_part[16 * i : 16 * i + 16, j * c_width : (j + 1) * c_width]
-        r_r[me_row] = r_s[me_row]
-        wait_r = exchange(6, lambda s: r_s.at[s], r_r, "plane")
+
+        l_pad[...] = jnp.zeros_like(l_pad)
+        l_pad[0:rpc, :] = l_s[...]
+        g_part = dot_nt(l_pad[...], whole_left, HIGHEST)[:rpc]
+        z_part = unstacked(dot_nt(stacked(l_pad[...]), cot_rows))[:rpc] * grad_scale
+        for k in range(plane):
+            g_s[k] = jnp.concatenate([g_part, z_part[:, k * t_act : (k + 1) * t_act]], axis=1)
+        g_r[me_row] = g_s[me_row]
+        wait_g = exchange(4, lambda s: g_s.at[s], g_r, "plane")
+        left_m = fold3(dot_nn(jnp.concatenate(split3(whole_left), axis=0), m[...]))
+        s_m[...] = left_m
+        advance(T[3])
         finish((3, 4))
 
         loads[7].wait()
@@ -413,13 +376,24 @@
             device_id_type=MESH,
         )
         to_pair.start()
-        wait_r.wait()
-        r_m[...] = jnp.sum(r_r[...].astype(F32), axis=0).astype(BF16)
-        r_g[me_row] = r_m[...]
-        wait_rg = exchange(8, lambda s: r_m, r_g, "plane")
+        advance(T[4])
+        wait_g.wait()
+        g_m[...] = jnp.sum(g_r[...], axis=0)
+        g_g[me_col] = g_m[...]
+        wait_gg = exchange(5, lambda s: g_m, g_g, "col")
+
+        def turned(i, carry):
+            at = pl.multiple_of(i * t_cot, t_cot)
+            c_t[:, pl.ds(at, t_cot)] = c_all[i].T
+            return carry
+
+        lax.fori_loop(0, cols, turned, 0)
         to_pair.wait_recv()
         for k in range(nz):
             q_s[k] = (p_s[c, k].astype(F32) + p_r[k].astype(F32)).astype(BF16)
+        q_r[z] = q_s[z]
+        advance(T[5])
+        wait_gg.wait()
 
         def send_q(k, carry):
             pz = (z + k) % nz
@@ -433,11 +407,51 @@
             ).start()
             return carry
 
-        q_r[z] = q_s[z]
         lax.fori_loop(1, nz, send_q, 0)
         q_part = q_r.at[pl.ds(0, nz - 1)]
         wait_q = pltpu.make_async_copy(q_part, q_part, small_recv.at[9])
         drains.append(pltpu.make_async_copy(q_part, q_part, small_send.at[9]))
+        for k in range(cols):
+            gram[k * rpc : (k + 1) * rpc, :] = g_g[k]
+        gram_z = gram[...]
+        z3 = jnp.concatenate(split3(gram_z[:, RANK:]), axis=0)
+        s_m[:, ky] = s_m[:, ky] + fold3(dot_nn(z3, a_y[me_row]))
+        s_m[:, kx] = s_m[:, kx] + fold3(dot_nn(z3, a_x[me_row]))
+
+        sub = lax.broadcasted_iota(jnp.int32, (RANK, 128), 0)
+        lan = lax.broadcasted_iota(jnp.int32, (RANK, 128), 1)
+        aug = jnp.where(lan < RANK, gram_z, jnp.where(lan - RANK == sub, 1.0, 0.0))
+        bands = [aug[8 * k : 8 * k + 8] for k in range(RANK // 8)]
+        sub_band = lax.broadcasted_iota(jnp.int32, (8, 128), 0)
+        for j in range(RANK - 1):
+            top, at = divmod(j, 8)
+            row = bands[top][at : at + 1, :]
+            row_over = row * (1.0 / row[:, j : j + 1])
+            for k in range((j + 1) // 8, RANK // 8):
+                step_down = bands[k][:, j : j + 1] * row_over
+                if k == top:
+                    step_down = jnp.where(sub_band > at, step_down, 0.0)
+                bands[k] = bands[k] - step_down
+            if j % 16 == 15:
+                advance(T[5] + (T[6] - T[5]) * (j + 1) / RANK)
+        aug = jnp.concatenate(bands, axis=0)
+        pivot = jnp.sum(jnp.where(lan == sub, aug, 0.0), axis=1, keepdims=True)
+        inverse = aug[:, RANK:] / jnp.sqrt(pivot)
+
+        r_part = dot_nn(inverse, s_m[...], HIGHEST).astype(BF16)
+        for i in range(r_groups):
+            for j in range(c_groups):
+                r_s[i * c_groups + j] = r_part[16 * i : 16 * i + 16, j * c_width : (j + 1) * c_width]
+        r_r[me_row] = r_s[me_row]
+        wait_r = exchange(6, lambda s: r_s.at[s], r_r, "plane")
+        orth[...] = dot_nn(inverse, whole_left, HIGHEST)
+        o_both[...] = jnp.concatenate(split2(orth[...]), axis=0)
+        advance(T[7])
+        wait_r.wait()
+        r_m[...] = jnp.sum(r_r[...].astype(F32), axis=0).astype(BF16)
+        r_g[me_row] = r_m[...]
+        wait_rg = exchange(8, lambda s: r_m, r_g, "plane")
+        advance(T[8])
         wait_rg.wait()
         for i in range(r_groups):
             for j in range(c_groups):
@@ -456,11 +470,21 @@
         y_r[me_col] = y_s[me_col]
         wait_y = exchange(11, lambda s: y_s.at[s], y_r, "col")
 
+        finish((0, 1))
         both = jnp.concatenate([right, right], axis=0)
-
-
-        feed = dot_tn(o_both, both)
-        m_out[...] = (buf[...] - feed_scale * feed).astype(BF16)
+        gathered_y = a_y[...].reshape(tokens, wy)
+        gathered_x = a_x[...].reshape(tokens, wx)
+        block = min(128, rows)
+
+        def momentum_block(i, carry):
+            at = pl.ds(pl.multiple_of(i * block, block), block)
+            lhs, low_rank = c_t[at, :], o_both[:, at]
+            for cut, gathered, part in ((ky, gathered_y, both[:, :wy]), (kx, gathered_x, both[:, wy:])):
+                value = m[at, cut].astype(F32) + grad_scale * dot_nn(lhs, gathered)
+                m_out[at, cut] = (value - feed_scale * dot_tn(low_rank, part)).astype(BF16)
+            return carry
+
+        lax.fori_loop(0, rows // block, momentum_block, 0)
 
         wait_s.wait()
         total = jnp.sum(s_r[...], axis=0)[0:1]
@@ -495,9 +519,9 @@
         vmem((rows, width), BF16),
         vmem((rows, width), BF16),
         vmem((RANK, width), F32),
-        vmem((rows, width), F32),
-        vmem((rows, width), BF16),
-        vmem((rows, width), BF16),
+        vmem((RANK, width), F32),
+        vmem((sub8, rows), F32),
+        vmem((2 * RANK, rows), BF16),
         vmem((cols, rpc, 128), F32),
         vmem((cols, rpc, 128), F32),
         vmem((cols, rpc, rows), F32),
@@ -508,7 +532,7 @@
         vmem((rpc, rows), F32),
         vmem((cols, rpc, rows), F32),
         vmem((RANK, rows), F32),
-        vmem((rpc, 128), F32),
+        vmem((plane, rpc, 128), F32),
         vmem((plane, rpc, 128), F32),
         vmem((rpc, 128), F32),
         vmem((cols, rpc, 128), F32),
@@ -541,7 +565,7 @@
             jax.ShapeDtypeStruct((RANK, width), F32),
             jax.ShapeDtypeStruct((n_out, rows), BF16),
         ),
-        in_specs=[pl.BlockSpec(memory_space=pl.ANY)] * 6,
+        in_specs=[pl.BlockSpec(memory_space=pltpu.HBM)] * 6,
         out_specs=[pl.BlockSpec(memory_space=pltpu.VMEM)] * 4,
         scratch_shapes=scratch,
         compiler_params=pltpu.CompilerParams(
@@ -550,13 +574,35 @@
     )
 
 
+def placed(values):
+    count = len(values)
+
+    def kernel(*refs):
+        sems = refs[-1]
+        copies = [pltpu.make_async_copy(refs[k], refs[count + k], sems.at[k]) for k in range(count)]
+        for copy in copies:
+            copy.start()
+        for copy in copies:
+            copy.wait()
+
+    return pl.pallas_call(
+        kernel,
+        out_shape=tuple(jax.ShapeDtypeStruct(v.shape, v.dtype) for v in values),
+        in_specs=[pl.BlockSpec(memory_space=pltpu.VMEM)] * count,
+        out_specs=[pl.BlockSpec(memory_space=pl.ANY)] * count,
+        scratch_shapes=[pltpu.SemaphoreType.DMA((count,))],
+        compiler_params=pltpu.CompilerParams(vmem_limit_bytes=8 * 1024 * 1024),
+    )(*values)
+
+
 def solution(mesh, sizes=(4, 8, 8, 2)):
     torus = Mesh(mesh.devices.reshape(sizes), ("x", "y", "z", "c"))
     row, col = ("x", "y"), ("z", "c")
 
     def body(activations, cotangents, weights, momentum, right_basis, next_inputs):
         shapes = dict(act=activations.shape, cot=cotangents.shape, nxt=next_inputs.shape)
-        return build(torus, shapes)(activations, cotangents, weights, momentum, right_basis, next_inputs)
+        results = build(torus, shapes)(activations, cotangents, weights, momentum, right_basis, next_inputs)
+        return placed(results)
 
     return jax.shard_map(
         body,

time: 120 us -> 111 us (0.925)
  Pallas kernels: 114 us -> 106 us
    pallas_call x1, Pallas kernels: 114 us -> 105 us  [body(): build(torus, shapes)]
    pallas_call x0 -> x1, Pallas kernels: none -> 1.44 us  [placed(): pl.pallas_call(kernel, out_shape=tuple((jax.ShapeDtypeStruct(v.shape, v.d...]
    unnamed x10 -> x8, local copies, waits for them, and re-layouts: 4.94 us -> 4.23 us
where the time goes in v2:
time: 111 us
  Pallas kernels  106 us (95%)
  local copies, waits for them, and re-layouts  4.23 us (4%)
    pallas_call x1, Pallas kernels, body(): build(torus, shapes)  105 us
    unnamed x8, local copies, waits for them, and re-layouts  4.23 us

profile of v2, /device:TPU:1, one launch (start us, length us, event | category | flops | bytes accessed | tf_op | source)
XLA Modules:
  0.0 111.1 jit_solution(15898939930322157347)
XLA Ops:
  0.6 104.8 %shard_map.93 = (bf16[512,1024]{1,0:T(8,128)(2,1)}, bf16[512,1024]{1,0:T(8,128)(2,1)}, f32[64,1024]{1,0:T(8,128)}, bf16[64,512]{1,0:T(8,128)(2,1)}) custom-call(bf16[64,1024]{1,0:T(8,128)(2,1)} %act.1, bf16[128,512]{1,0:T(8,128)(2,1)} %cot.1, bf16[512,1024]{1,0:T(8,128)(2,1)} %w_in.1, bf16[512,1024]{1,0:T(8,128)(2,1)} %m_in.1, f32[64,1024]{1,0:T(8,128)} %rb.1, ...), custom_call_target="tpu_custom_call" | custom-call | tf_op jit(solution)/shard_map/pallas_call | solution.py:604
  105.4 0.0 copy-start
  105.4 1.2 %copy-done = bf16[512,1024]{1,0:T(8,128)(2,1)S(1)} copy-done((bf16[512,1024]{1,0:T(8,128)(2,1)S(1)}, bf16[512,1024]{1,0:T(8,128)(2,1)}, u32[]{:S(2)}) %copy-start) | copy-done | bytes 1048600
  106.6 0.0 copy-start.1
  106.6 1.2 %copy-done.1 = bf16[512,1024]{1,0:T(8,128)(2,1)S(1)} copy-done((bf16[512,1024]{1,0:T(8,128)(2,1)S(1)}, bf16[512,1024]{1,0:T(8,128)(2,1)}, u32[]{:S(2)}) %copy-start.1) | copy-done | bytes 1048600
  107.9 0.0 copy-start.2
  107.9 0.9 copy-done.2
  108.8 0.0 copy-start.3
  108.8 0.8 copy-done.3
  109.7 1.4 %shard_map.94 = (bf16[512,1024]{1,0:T(8,128)(2,1)}, bf16[512,1024]{1,0:T(8,128)(2,1)}, f32[64,1024]{1,0:T(8,128)}, bf16[64,512]{1,0:T(8,128)(2,1)}) custom-call(bf16[512,1024]{1,0:T(8,128)(2,1)S(1)} %copy-done, bf16[512,1024]{1,0:T(8,128)(2,1)S(1)} %copy-done.1, f32[64,1024]{1,0:T(8,128)S(1)} %copy-done.2, bf16[64,512]{1,0:T(8,128)(2,1)S(1)} %copy-done.3), custom_call_target="tpu_custom_call" | custom-call | tf_op jit(solution)/shard_map/pallas_call | solution.py:588
Async XLA Ops:
  105.4 1.2 %copy-start = (bf16[512,1024]{1,0:T(8,128)(2,1)S(1)}, bf16[512,1024]{1,0:T(8,128)(2,1)}, u32[]{:S(2)}) copy-start(bf16[512,1024]{1,0:T(8,128)(2,1)} %get-tuple-element.8.refs_0_) | copy-start | bytes 3145732
  106.6 1.2 %copy-start.1 = (bf16[512,1024]{1,0:T(8,128)(2,1)S(1)}, bf16[512,1024]{1,0:T(8,128)(2,1)}, u32[]{:S(2)}) copy-start(bf16[512,1024]{1,0:T(8,128)(2,1)} %get-tuple-element.9.refs_1_) | copy-start | bytes 3145732
  107.9 0.9 copy-start.2
  108.8 0.8 copy-start.3

commit v3 on v2

--- a/solution.py
+++ b/solution.py
@@ -361,12 +361,14 @@
         per = n_out // n_next
 
         def product_block(i, carry):
-            at = pl.ds(i * per, per)
-            value = dot_nt(n_y[at].reshape(n_out, wy), w[:, :wy]) + dot_nt(n_x[at].reshape(n_out, wx), w[:, wy:])
-            p_s[i % nc, i // nc] = (value * out_scale).astype(BF16)
+            at = pl.ds(i * 4 * per, 4 * per)
+            value = dot_nt(n_y[at].reshape(4 * n_out, wy), w[:, :wy])
+            value = value + dot_nt(n_x[at].reshape(4 * n_out, wx), w[:, wy:])
+            for j in range(4):
+                p_s[j % nc, i * (4 // nc) + j // nc] = (value[j * n_out : (j + 1) * n_out] * out_scale).astype(BF16)
             return carry
 
-        lax.fori_loop(0, cols, product_block, 0)
+        lax.fori_loop(0, cols // 4, product_block, 0)
         to_pair = pltpu.make_async_remote_copy(
             src_ref=p_s.at[1 - c],
             dst_ref=p_r,
@@ -578,20 +580,24 @@
     count = len(values)
 
     def kernel(*refs):
-        sems = refs[-1]
-        copies = [pltpu.make_async_copy(refs[k], refs[count + k], sems.at[k]) for k in range(count)]
-        for copy in copies:
+        stage, sems = refs[2 * count : 3 * count], refs[-1]
+        taken = [pltpu.make_async_copy(refs[k], stage[k], sems.at[0, k]) for k in range(count)]
+        given = [pltpu.make_async_copy(stage[k], refs[count + k], sems.at[1, k]) for k in range(count)]
+        for copy in taken:
             copy.start()
-        for copy in copies:
+        for k in range(count):
+            taken[k].wait()
+            given[k].start()
+        for copy in given:
             copy.wait()
 
     return pl.pallas_call(
         kernel,
         out_shape=tuple(jax.ShapeDtypeStruct(v.shape, v.dtype) for v in values),
-        in_specs=[pl.BlockSpec(memory_space=pltpu.VMEM)] * count,
+        in_specs=[pl.BlockSpec(memory_space=pl.ANY)] * count,
         out_specs=[pl.BlockSpec(memory_space=pl.ANY)] * count,
-        scratch_shapes=[pltpu.SemaphoreType.DMA((count,))],
-        compiler_params=pltpu.CompilerParams(vmem_limit_bytes=8 * 1024 * 1024),
+        scratch_shapes=[pltpu.VMEM(v.shape, v.dtype) for v in values] + [pltpu.SemaphoreType.DMA((2, count))],
+        compiler_params=pltpu.CompilerParams(vmem_limit_bytes=60 * 1024 * 1024),
     )(*values)
 
 

time: 111 us -> 103 us (0.928)
  local copies, waits for them, and re-layouts: 4.23 us -> 0 us
  Pallas kernels: 106 us -> 103 us
    pallas_call x1, Pallas kernels: 105 us -> 99.8 us  [body(): build(torus, shapes)]
    unnamed x8 -> x0, local copies, waits for them, and re-layouts: 4.23 us -> none
    pallas_call x1, Pallas kernels: 1.44 us -> 2.7 us  [placed(): pl.pallas_call(kernel, out_shape=tuple((jax.ShapeDtypeStruct(v.shape, v.d...]
where the time goes in v3:
time: 103 us
  Pallas kernels  103 us (100%)
    pallas_call x1, Pallas kernels, body(): build(torus, shapes)  99.8 us
    pallas_call x1, Pallas kernels, placed(): pl.pallas_call(kernel, out_shape=tuple((jax.ShapeDtypeStruct(v.shape, v.d...  2.7 us

profile of v3, /device:TPU:1, one launch (start us, length us, event | category | flops | bytes accessed | tf_op | source)
XLA Modules:
  0.0 103.2 jit_solution(12051357655259636341)
XLA Ops:
  0.6 99.8 %shard_map.93 = (bf16[512,1024]{1,0:T(8,128)(2,1)}, bf16[512,1024]{1,0:T(8,128)(2,1)}, f32[64,1024]{1,0:T(8,128)}, bf16[64,512]{1,0:T(8,128)(2,1)}) custom-call(bf16[64,1024]{1,0:T(8,128)(2,1)} %act.1, bf16[128,512]{1,0:T(8,128)(2,1)} %cot.1, bf16[512,1024]{1,0:T(8,128)(2,1)} %w_in.1, bf16[512,1024]{1,0:T(8,128)(2,1)} %m_in.1, f32[64,1024]{1,0:T(8,128)} %rb.1, ...), custom_call_target="tpu_custom_call" | custom-call | tf_op jit(solution)/shard_map/pallas_call | solution.py:610
  100.4 2.7 %shard_map.94 = (bf16[512,1024]{1,0:T(8,128)(2,1)}, bf16[512,1024]{1,0:T(8,128)(2,1)}, f32[64,1024]{1,0:T(8,128)}, bf16[64,512]{1,0:T(8,128)(2,1)}) custom-call(bf16[512,1024]{1,0:T(8,128)(2,1)} %get-tuple-element.8.refs_0_, bf16[512,1024]{1,0:T(8,128)(2,1)} %get-tuple-element.9.refs_1_, f32[64,1024]{1,0:T(8,128)} %get-tuple-element.10.refs_2_, ...), custom_call_target="tpu_custom_call" | custom-call | tf_op jit(solution)/shard_map/pallas_call | solution.py:594
